TPU v7x, 32 devices: a whole 2x2x4 slice. The times are simulated.
32 devices in a mesh: owner: 8 (over z, y), rows: 4 (over x, core).
Axes of the slice: x: 2, y: 2, z: 4, core: 2. Of those that a mesh axis runs over, the one named last changes fastest.
Arguments:
- master_down: float32 [16, 6400, 4096], P('owner', None, 'rows'), may hold values from -0.109375 to 0.109375
- router_weight: float32 [4096, 16], P('rows', 'owner'), may hold values from -0.09375 to 0.09375
- router_gain: float32 [4096], P('rows'), may hold values from 0.25 to 1.75
Outputs:
- final_down: bfloat16 [16, 6400, 4096], P('owner', 'rows')
- scale_down: float32 [16, 6400], P('owner', 'rows')
- serve_router: bfloat16 [4096, 16], replicated
All inputs are finite; a program needn't handle non-finite values. Where the computation divides by a largest or mean magnitude, that divisor is 1e-20 or more.
Results may differ from a plain program's by a relative error of at most 0.001.
Values may be sent and summed in bfloat16 or wider, within the bound.
A program may use at most 192 MiB of HBM per device.

v0:
```python
import jax
import jax.numpy as jnp
from jax import lax
from jax.sharding import PartitionSpec as P

D_MODEL = 4096


def per_device(master_down, router_weight, router_gain):
    total_down = lax.psum(jnp.sum(jnp.abs(master_down), axis=2), "rows")
    scale_down = total_down / D_MODEL
    narrow_down = (master_down / jnp.expand_dims(scale_down, 2)).astype(jnp.bfloat16)
    final_down = lax.all_to_all(narrow_down, "rows", split_axis=1, concat_axis=2, tiled=True)
    scale_down = lax.dynamic_slice_in_dim(
        scale_down, lax.axis_index("rows") * final_down.shape[1], final_down.shape[1], axis=1
    )
    part_router = (router_weight * router_gain[:, None]).astype(jnp.bfloat16)
    row_router = lax.all_gather(part_router, "rows", axis=0, tiled=True)
    serve_router = lax.all_gather(row_router, "owner", axis=1, tiled=True)
    return (final_down, scale_down, serve_router)


def solution(mesh):
    return jax.shard_map(
        per_device,
        mesh=mesh,
        in_specs=(P("owner", None, "rows"), P("rows", "owner"), P("rows")),
        out_specs=(P("owner", "rows", None), P("owner", "rows"), P()),
        check_vma=False,
    )
```

profile of v0, /device:TPU:0, one launch (start us, length us, event | category | flops | bytes accessed | tf_op | source)
XLA Modules:
  0.0 506.3 jit_solution(15090514093543817720)
XLA Ops:
  0.6 17.0 %abs_reduce_fusion = f32[2,6400]{1,0:T(2,128)S(1)} fusion(f32[2,6400,1024]{2,1,0:T(8,128)} %param.3), kind=kLoop, calls=%fused_computation.1 | loop fusion | flops 26201600 | bytes 52480000 | tf_op jit(solution)/shard_map/reduce_sum | solution.py:10
  17.6 13.4 %psum.7 = f32[2,6400]{1,0:T(2,128)S(1)} all-reduce(f32[2,6400]{1,0:T(2,128)S(1)} %abs_reduce_fusion), channel_id=1, replica_groups=mesh['owner'=8,'rows'=4] {'rows'}, use_global_device_ids=true, to_apply=%region_1.0 | all-reduce | flops 12800 | bytes 102400 | tf_op jit(solution)/shard_map/psum | solution.py:10
  31.1 26.1 %divide_convert_fusion = bf16[2,6400,1024]{2,1,0:T(8,128)(2,1)} fusion(f32[2,6400,1024]{2,1,0:T(8,128)} %param.3, f32[2,6400]{1,0:T(2,128)S(1)} %broadcast_multiply_fusion), kind=kLoop, calls=%fused_computation | loop fusion | flops 26214400 | bytes 78694400 | tf_op jit(solution)/shard_map/convert_element_type | solution.py:12
  57.2 0.0 copy-start
  57.2 0.0 copy-start.1
  57.2 47.4 %copy.10 = bf16[2,6400,1024]{2,0,1:T(2,128)(2,1)} copy(bf16[2,6400,1024]{2,1,0:T(8,128)(2,1)} %divide_convert_fusion) | data formatting | bytes 52428800 | tf_op jit(solution)/shard_map/convert_element_type | solution.py:12
  104.6 8.6 %all-to-all-start = ((bf16[2,6400,1024]{2,0,1:T(2,128)(2,1)}), bf16[2,6400,1024]{2,0,1:T(2,128)(2,1)}, u32[]{:S(2)}, u32[]{:S(2)}) async-start(bf16[2,6400,1024]{2,0,1:T(2,128)(2,1)} %copy.10), calls=%async_computation | async-start | bytes 52428800 | tf_op jit(solution)/shard_map/all_to_all | solution.py:13
  113.2 0.0 copy-done
  113.2 0.0 copy-done.1
  113.2 285.0 %all_gather.6 = bf16[4096,2]{0,1:T(2,128)(2,1)S(1)} all-gather(bf16[1024,2]{0,1:T(2,128)(2,1)S(1)} %multiply_convert_fusion), channel_id=1, replica_groups=mesh['owner'=8,'rows'=4] {'rows'}, dimensions={0}, use_global_device_ids=true | all-gather | bytes 20480 | tf_op jit(solution)/shard_map/all_gather | solution.py:18
  398.2 30.9 %all-gather = bf16[8,2,4096]{2,1,0:T(2,128)(2,1)S(1)} all-gather(bf16[1,2,4096]{2,1,0:T(2,128)(2,1)S(1)} %bitcast.8), channel_id=1, replica_groups=mesh['owner'=8,'rows'=4] {'owner'}, dimensions={0}, use_global_device_ids=true | all-gather | bytes 147456 | tf_op jit(solution)/shard_map/all_gather | solution.py:19
  429.1 0.7 reshape.9
  429.8 0.7 constant_dynamic-slice_fusion
  430.5 0.0 all-to-all-done
  430.5 33.4 %copy.11 = bf16[2,1600,4,1024]{3,2,1,0:T(4,128)(2,1)} copy(bf16[2,1600,4,1024]{3,0,1,2:T(2,128)(2,1)} %bitcast.1) | data formatting | bytes 52428800 | tf_op jit(solution)/shard_map/all_to_all | solution.py:13
  463.9 42.5 %all_to_all.16 = bf16[2,1600,4096]{2,1,0:T(8,128)(2,1)} reshape(bf16[2,1600,4,1024]{3,2,1,0:T(4,128)(2,1)} %copy.11) | data formatting | bytes 52428800 | tf_op jit(solution)/shard_map/all_to_all | solution.py:13
  (2 shorter events, 0.0 us)
Async XLA Ops:
  57.2 56.0 %copy-start = (f32[1024,2]{0,1:T(2,128)S(1)}, f32[1024,2]{0,1:T(2,128)}, u32[]{:S(2)}) copy-start(f32[1024,2]{0,1:T(2,128)} %param.4) | copy-start | bytes 24580
  57.2 56.0 %copy-start.1 = (f32[1024]{0:T(1024)S(1)}, f32[1024]{0:T(1024)}, u32[]{:S(2)}) copy-start(f32[1024]{0:T(1024)} %param.5) | copy-start | bytes 12292
  104.6 325.9 %all-to-all-start = ((bf16[2,6400,1024]{2,0,1:T(2,128)(2,1)}), bf16[2,6400,1024]{2,0,1:T(2,128)(2,1)}, u32[]{:S(2)}, u32[]{:S(2)}) async-start(bf16[2,6400,1024]{2,0,1:T(2,128)(2,1)} %copy.10), calls=%async_computation | async-start | bytes 52428800 | tf_op jit(solution)/shard_map/all_to_all | solution.py:13
where the time goes:
time: 508 us; the launch traced here: 506 us
  blocking collectives  329 us (65%)
  local copies, waits for them, and re-layouts  125 us (25%)
  other arithmetic  43.2 us (9%)
  starting transfers between devices  8.59 us (2%)
    all_gather x1, blocking collectives, per_device(): row_router = lax.all_gather(part_router, 'rows', axis=0, tiled=True)  285 us
    all_to_all x2, local copies, waits for them, and re-layouts, per_device(): lax.all_to_all(narrow_down, 'rows', split_axis=1, concat_axis=2, tiled=True)  75.8 us
    convert_element_type x1, local copies, waits for them, and re-layouts, per_device(): (master_down / jnp.expand_dims(scale_down, 2)).astype(jnp.bfloat16)  47.4 us
    all_gather x1, blocking collectives, per_device(): serve_router = lax.all_gather(row_router, 'owner', axis=1, tiled=True)  30.9 us
    convert_element_type x1, other arithmetic, per_device(): (master_down / jnp.expand_dims(scale_down, 2)).astype(jnp.bfloat16)  26.1 us
    reduce_sum x1, other arithmetic, per_device(): total_down = lax.psum(jnp.sum(jnp.abs(master_down), axis=2), 'rows')  17 us
    psum x1, blocking collectives, per_device(): total_down = lax.psum(jnp.sum(jnp.abs(master_down), axis=2), 'rows')  13.4 us
  transfers between devices with their start and end apart: 1, of which 0 were waited for; matrix products, arithmetic and copies ran while one was open for 0% of the time, Pallas kernels for 0%

commit v1 on v0

--- a/solution.py
+++ b/solution.py
@@ -2,15 +2,23 @@
 import jax.numpy as jnp
 from jax import lax
 from jax.sharding import PartitionSpec as P
+from jax.lax import all_to_all, axis_size
 
 D_MODEL = 4096
+
+
+def view_cube(mesh_dim, a0):
+    field_out = jnp.split(a0, axis_size(mesh_dim), axis=1)
+    carry_out = jnp.stack(field_out)
+    state_next = all_to_all(carry_out, mesh_dim, 0, 0)
+    return jnp.concatenate(state_next, axis=2)
 
 
 def per_device(master_down, router_weight, router_gain):
     total_down = lax.psum(jnp.sum(jnp.abs(master_down), axis=2), "rows")
     scale_down = total_down / D_MODEL
     narrow_down = (master_down / jnp.expand_dims(scale_down, 2)).astype(jnp.bfloat16)
-    final_down = lax.all_to_all(narrow_down, "rows", split_axis=1, concat_axis=2, tiled=True)
+    final_down = view_cube("rows", narrow_down)
     scale_down = lax.dynamic_slice_in_dim(
         scale_down, lax.axis_index("rows") * final_down.shape[1], final_down.shape[1], axis=1
     )

time: 508 us -> 425 us (0.84)
  local copies, waits for them, and re-layouts: 125 us -> 32.6 us
  other arithmetic: 43.2 us -> 53.7 us
    all_to_all x2 -> x0, local copies, waits for them, and re-layouts: 75.8 us -> none  [per_device(): lax.all_to_all(narrow_down, 'rows', split_axis=1, concat_axis=2, tiled=True)]
    convert_element_type x1 -> x0, local copies, waits for them, and re-layouts: 47.4 us -> none  [per_device(): (master_down / jnp.expand_dims(scale_down, 2)).astype(jnp.bfloat16)]
    reshape x0 -> x1, local copies, waits for them, and re-layouts: none -> 21.7 us  [view_cube(): return jnp.concatenate(state_next, axis=2)]
    another operation x0 -> x1, other arithmetic: none -> 10.5 us  [view_cube(): carry_out = jnp.stack(field_out)]
    another operation x0 -> x1, local copies, waits for them, and re-layouts: none -> 9.52 us  [view_cube(): carry_out = jnp.stack(field_out)]
where the time goes in v1:
time: 425 us
  blocking collectives  329 us (77%)
  other arithmetic  53.7 us (13%)
  local copies, waits for them, and re-layouts  32.6 us (8%)
  starting transfers between devices  8.72 us (2%)
    all_gather x1, blocking collectives, per_device(): row_router = lax.all_gather(part_router, 'rows', axis=0, tiled=True)  285 us
    all_gather x1, blocking collectives, per_device(): serve_router = lax.all_gather(row_router, 'owner', axis=1, tiled=True)  30.9 us
    convert_element_type x1, other arithmetic, per_device(): (master_down / jnp.expand_dims(scale_down, 2)).astype(jnp.bfloat16)  26.1 us
    reshape x1, local copies, waits for them, and re-layouts, view_cube(): return jnp.concatenate(state_next, axis=2)  21.7 us
    reduce_sum x1, other arithmetic, per_device(): total_down = lax.psum(jnp.sum(jnp.abs(master_down), axis=2), 'rows')  17 us
    psum x1, blocking collectives, per_device(): total_down = lax.psum(jnp.sum(jnp.abs(master_down), axis=2), 'rows')  13.4 us
    another operation x1, other arithmetic, view_cube(): carry_out = jnp.stack(field_out)  10.5 us
    another operation x1, local copies, waits for them, and re-layouts, view_cube(): carry_out = jnp.stack(field_out)  9.52 us
  transfers between devices with their start and end apart: 1, of which 0 were waited for; matrix products, arithmetic and copies ran while one was open for 0% of the time, Pallas kernels for 0%

profile of v1, /device:TPU:0, one launch (start us, length us, event | category | flops | bytes accessed | tf_op | source)
XLA Modules:
  0.0 425.0 jit_solution(6237450179818523184)
XLA Ops:
  0.6 17.0 %abs_reduce_fusion = f32[2,6400]{1,0:T(2,128)S(1)} fusion(f32[2,6400,1024]{2,1,0:T(8,128)} %param.3), kind=kLoop, calls=%fused_computation.1 | loop fusion | flops 26201600 | bytes 52480000 | tf_op jit(solution)/shard_map/reduce_sum | solution.py:18
  17.6 13.4 %psum.7 = f32[2,6400]{1,0:T(2,128)S(1)} all-reduce(f32[2,6400]{1,0:T(2,128)S(1)} %abs_reduce_fusion), channel_id=1, replica_groups=mesh['owner'=8,'rows'=4] {'rows'}, use_global_device_ids=true, to_apply=%region_1.0 | all-reduce | flops 12800 | bytes 102400 | tf_op jit(solution)/shard_map/psum | solution.py:18
  31.1 26.1 %divide_convert_fusion = bf16[2,6400,1024]{2,1,0:T(8,128)(2,1)} fusion(f32[2,6400,1024]{2,1,0:T(8,128)} %param.3, f32[2,6400]{1,0:T(2,128)S(1)} %broadcast_multiply_fusion), kind=kLoop, calls=%fused_computation | loop fusion | flops 26214400 | bytes 78694400 | tf_op jit(solution)/shard_map/convert_element_type | solution.py:20
  57.2 9.5 %slice_bitcast_fusion.3 = (bf16[1,2,1600,1024]{3,2,1,0:T(8,128)(2,1)S(1)}, bf16[1,2,1600,1024]{3,2,1,0:T(8,128)(2,1)S(1)}, bf16[1,2,1600,1024]{3,2,1,0:T(8,128)(2,1)S(1)}, bf16[1,2,1600,1024]{3,2,1,0:T(8,128)(2,1)S(1)}) fusion(bf16[2,6400,1024]{2,1,0:T(8,128)(2,1)} %divide_convert_fusion), kind=kLoop, calls=%fused_computation.6 | loop fusion | bytes 52428800 | tf_op jit(solution)/shard_map/stack | solution.py:12
  66.7 10.5 %pad_maximum_fusion = bf16[4,2,1600,1024]{3,2,1,0:T(8,128)(2,1)} fusion(bf16[1,2,1600,1024]{3,2,1,0:T(8,128)(2,1)S(1)} %get-tuple-element.4, bf16[1,2,1600,1024]{3,2,1,0:T(8,128)(2,1)S(1)} %get-tuple-element.5, bf16[1,2,1600,1024]{3,2,1,0:T(8,128)(2,1)S(1)} %get-tuple-element.6, bf16[1,2,1600,1024]{3,2,1,0:T(8,128)(2,1)S(1)} %get-tuple-element.3), kind=kLoop, calls=%fused_computation.2 | loop fusion | flops 39321600 | bytes 52428800 | tf_op jit(solution)/shard_map/stack | solution.py:12
  77.3 0.0 copy-start
  77.3 0.0 copy-start.1
  77.3 8.7 %all-to-all-start = ((bf16[4,2,1600,1024]{3,2,1,0:T(8,128)(2,1)}), bf16[4,2,1600,1024]{3,2,1,0:T(8,128)(2,1)}, u32[]{:S(2)}, u32[]{:S(2)}) async-start(bf16[4,2,1600,1024]{3,2,1,0:T(8,128)(2,1)} %pad_maximum_fusion), calls=%async_computation | async-start | bytes 52428800 | tf_op jit(solution)/shard_map/all_to_all | solution.py:13
  86.0 0.0 copy-done
  86.0 0.0 copy-done.1
  86.0 285.0 %all_gather.6 = bf16[4096,2]{0,1:T(2,128)(2,1)S(1)} all-gather(bf16[1024,2]{0,1:T(2,128)(2,1)S(1)} %multiply_convert_fusion), channel_id=1, replica_groups=mesh['owner'=8,'rows'=4] {'rows'}, dimensions={0}, use_global_device_ids=true | all-gather | bytes 20480 | tf_op jit(solution)/shard_map/all_gather | solution.py:26
  371.1 30.9 %all-gather = bf16[8,2,4096]{2,1,0:T(2,128)(2,1)S(1)} all-gather(bf16[1,2,4096]{2,1,0:T(2,128)(2,1)S(1)} %bitcast.17), channel_id=1, replica_groups=mesh['owner'=8,'rows'=4] {'owner'}, dimensions={0}, use_global_device_ids=true | all-gather | bytes 147456 | tf_op jit(solution)/shard_map/all_gather | solution.py:27
  401.9 0.7 reshape.17
  402.6 0.7 constant_dynamic-slice_fusion
  403.3 0.0 all-to-all-done
  403.3 21.7 %copy.8 = bf16[4,2,200,8,1024]{4,3,0,2,1:T(8,128)(2,1)} copy(bf16[4,2,200,8,1024]{4,3,2,1,0:T(8,128)(2,1)} %bitcast.9) | data formatting | bytes 52428800 | tf_op jit(solution)/shard_map/reshape | solution.py:14
  (2 shorter events, 0.0 us)
Async XLA Ops:
  77.3 8.7 %copy-start = (f32[1024,2]{0,1:T(2,128)S(1)}, f32[1024,2]{0,1:T(2,128)}, u32[]{:S(2)}) copy-start(f32[1024,2]{0,1:T(2,128)} %param.4) | copy-start | bytes 24580
  77.3 8.7 %copy-start.1 = (f32[1024]{0:T(1024)S(1)}, f32[1024]{0:T(1024)}, u32[]{:S(2)}) copy-start(f32[1024]{0:T(1024)} %param.5) | copy-start | bytes 12292
  77.3 326.1 %all-to-all-start = ((bf16[4,2,1600,1024]{3,2,1,0:T(8,128)(2,1)}), bf16[4,2,1600,1024]{3,2,1,0:T(8,128)(2,1)}, u32[]{:S(2)}, u32[]{:S(2)}) async-start(bf16[4,2,1600,1024]{3,2,1,0:T(8,128)(2,1)} %pad_maximum_fusion), calls=%async_computation | async-start | bytes 52428800 | tf_op jit(solution)/shard_map/all_to_all | solution.py:13

commit v2 on v0

--- a/solution.py
+++ b/solution.py
@@ -15,7 +15,10 @@
         scale_down, lax.axis_index("rows") * final_down.shape[1], final_down.shape[1], axis=1
     )
     part_router = (router_weight * router_gain[:, None]).astype(jnp.bfloat16)
-    row_router = lax.all_gather(part_router, "rows", axis=0, tiled=True)
+    peers = lax.axis_size("rows")
+    pieces = jnp.stack([part_router for _ in range(peers)])
+    pieces = lax.all_to_all(pieces, "rows", split_axis=0, concat_axis=0)
+    row_router = jnp.concatenate(pieces, axis=0)
     serve_router = lax.all_gather(row_router, "owner", axis=1, tiled=True)
     return (final_down, scale_down, serve_router)
 

time: 508 us -> 479 us (0.943)
  blocking collectives: 329 us -> 43.7 us
  waiting for transfers between devices: 0.01 us -> 251 us
    all_gather x1 -> x0, blocking collectives: 285 us -> none  [per_device(): row_router = lax.all_gather(part_router, 'rows', axis=0, tiled=True)]
    all_to_all x1, waiting for transfers between devices: 0.01 us -> 251 us  [per_device(): lax.all_to_all(narrow_down, 'rows', split_axis=1, concat_axis=2, tiled=True)]
  transfers between devices with their start and end apart: 1 -> 2, of which waited for: 0 -> 1; matrix products, arithmetic and copies ran while one was open for 0% -> 19% of each run, Pallas kernels for 0% -> 0%
where the time goes in v2:
time: 479 us; the launch traced here: 478 us
  waiting for transfers between devices  251 us (52%)
  local copies, waits for them, and re-layouts  125 us (26%)
  other arithmetic  43.9 us (9%)
  blocking collectives  43.7 us (9%)
  starting transfers between devices  12.8 us (3%)
    all_to_all x1, waiting for transfers between devices, per_device(): lax.all_to_all(narrow_down, 'rows', split_axis=1, concat_axis=2, tiled=True)  251 us
    all_to_all x2, local copies, waits for them, and re-layouts, per_device(): lax.all_to_all(narrow_down, 'rows', split_axis=1, concat_axis=2, tiled=True)  75.8 us
    convert_element_type x1, local copies, waits for them, and re-layouts, per_device(): (master_down / jnp.expand_dims(scale_down, 2)).astype(jnp.bfloat16)  47.3 us
    all_gather x1, blocking collectives, per_device(): serve_router = lax.all_gather(row_router, 'owner', axis=1, tiled=True)  31.4 us
    convert_element_type x1, other arithmetic, per_device(): (master_down / jnp.expand_dims(scale_down, 2)).astype(jnp.bfloat16)  26.1 us
    reduce_sum x1, other arithmetic, per_device(): total_down = lax.psum(jnp.sum(jnp.abs(master_down), axis=2), 'rows')  17 us
    psum x1, blocking collectives, per_device(): total_down = lax.psum(jnp.sum(jnp.abs(master_down), axis=2), 'rows')  12.3 us
  transfers between devices with their start and end apart: 2, of which 1 were waited for; matrix products, arithmetic and copies ran while one was open for 19% of the time, Pallas kernels for 0%

profile of v2, /device:TPU:0, one launch (start us, length us, event | category | flops | bytes accessed | tf_op | source)
XLA Modules:
  0.0 477.7 jit_solution(16169897027497116059)
XLA Ops:
  0.6 0.7 multiply_convert_fusion
  1.3 0.6 stack.2
  2.0 4.2 all-to-all-start.1
  6.2 17.0 %abs_reduce_fusion = f32[2,6400]{1,0:T(2,128)S(1)} fusion(f32[2,6400,1024]{2,1,0:T(8,128)} %param.3), kind=kLoop, calls=%fused_computation.1 | loop fusion | flops 26201600 | bytes 52480000 | tf_op jit(solution)/shard_map/reduce_sum | solution.py:10
  23.2 12.3 %psum.7 = f32[2,6400]{1,0:T(2,128)S(1)} all-reduce(f32[2,6400]{1,0:T(2,128)S(1)} %abs_reduce_fusion), channel_id=1, replica_groups=mesh['owner'=8,'rows'=4] {'rows'}, use_global_device_ids=true, to_apply=%region_1.0 | all-reduce | flops 12800 | bytes 102400 | tf_op jit(solution)/shard_map/psum | solution.py:10
  35.6 26.1 %divide_convert_fusion = bf16[2,6400,1024]{2,1,0:T(8,128)(2,1)} fusion(f32[2,6400,1024]{2,1,0:T(8,128)} %param.3, f32[2,6400]{1,0:T(2,128)S(1)} %broadcast_multiply_fusion), kind=kLoop, calls=%fused_computation | loop fusion | flops 26214400 | bytes 78694400 | tf_op jit(solution)/shard_map/convert_element_type | solution.py:12
  61.7 47.3 %copy.10 = bf16[2,6400,1024]{2,0,1:T(2,128)(2,1)} copy(bf16[2,6400,1024]{2,1,0:T(8,128)(2,1)} %divide_convert_fusion) | data formatting | bytes 52428800 | tf_op jit(solution)/shard_map/convert_element_type | solution.py:12
  109.1 0.0 all-to-all-done.1
  109.1 8.6 %all-to-all-start = ((bf16[2,6400,1024]{2,0,1:T(2,128)(2,1)}), bf16[2,6400,1024]{2,0,1:T(2,128)(2,1)}, u32[]{:S(2)}, u32[]{:S(2)}) async-start(bf16[2,6400,1024]{2,0,1:T(2,128)(2,1)} %copy.10), calls=%async_computation | async-start | bytes 52428800 | tf_op jit(solution)/shard_map/all_to_all | solution.py:13
  117.7 0.7 constant_dynamic-slice_fusion
  118.4 31.4 %all-gather = bf16[8,2,4096]{2,1,0:T(2,128)(2,1)S(1)} all-gather(bf16[1,2,4096]{2,1,0:T(2,128)(2,1)S(1)} %bitcast.10), channel_id=1, replica_groups=mesh['owner'=8,'rows'=4] {'owner'}, dimensions={0}, use_global_device_ids=true | all-gather | bytes 147456 | tf_op jit(solution)/shard_map/all_gather | solution.py:22
  149.7 0.7 reshape.15
  150.5 251.4 %all-to-all-done = bf16[2,6400,1024]{2,0,1:T(2,128)(2,1)} async-done(((bf16[2,6400,1024]{2,0,1:T(2,128)(2,1)}), bf16[2,6400,1024]{2,0,1:T(2,128)(2,1)}, u32[]{:S(2)}, u32[]{:S(2)}) %all-to-all-start) | async-done | bytes 26214432 | tf_op jit(solution)/shard_map/all_to_all | solution.py:13
  401.8 33.3 %copy.11 = bf16[2,1600,4,1024]{3,2,1,0:T(4,128)(2,1)} copy(bf16[2,1600,4,1024]{3,0,1,2:T(2,128)(2,1)} %bitcast.1) | data formatting | bytes 52428800 | tf_op jit(solution)/shard_map/all_to_all | solution.py:13
  435.2 42.5 %all_to_all.19 = bf16[2,1600,4096]{2,1,0:T(8,128)(2,1)} reshape(bf16[2,1600,4,1024]{3,2,1,0:T(4,128)(2,1)} %copy.11) | data formatting | bytes 52428800 | tf_op jit(solution)/shard_map/all_to_all | solution.py:13
  (1 shorter events, 0.0 us)
Async XLA Ops:
  2.0 107.1 %all-to-all-start.1 = ((bf16[4,1024,2]{1,2,0:T(2,128)(2,1)}), bf16[4,1024,2]{1,2,0:T(2,128)(2,1)S(1)}, u32[]{:S(2)}, u32[]{:S(2)}) async-start(bf16[4,1024,2]{1,2,0:T(2,128)(2,1)} %stack.2), calls=%async_computation.1 | async-start | bytes 32768 | tf_op jit(solution)/shard_map/all_to_all | solution.py:20
  109.1 292.8 %all-to-all-start = ((bf16[2,6400,1024]{2,0,1:T(2,128)(2,1)}), bf16[2,6400,1024]{2,0,1:T(2,128)(2,1)}, u32[]{:S(2)}, u32[]{:S(2)}) async-start(bf16[2,6400,1024]{2,0,1:T(2,128)(2,1)} %copy.10), calls=%async_computation | async-start | bytes 52428800 | tf_op jit(solution)/shard_map/all_to_all | solution.py:13
